TPU v7x, 32 devices: a whole 2x2x4 slice. The times are simulated.
32 devices in a mesh: gy: 8 (over y, x, core), gx: 4 (over z).
Axes of the slice: x: 2, y: 2, z: 4, core: 2. Of those that a mesh axis runs over, the one named last changes fastest.
Arguments:
- tracer: float32 [8, 1024, 1024], P(None, 'gy', 'gx'), may hold values from -6 to 6
- east_speed: float32 [8, 1024, 1024], P(None, 'gy', 'gx'), may hold values from -0.25 to 0.25
- north_speed: float32 [8, 1024, 1024], P(None, 'gy', 'gx'), may hold values from -0.25 to 0.25
- columns: int32 [1024, 1024], P('gy', 'gx'), may hold values from 0 to 8
- thickness: float32 [8], replicated, may hold values from 0.5 to 2
- surface_flux: float32 [1024, 1024], P('gy', 'gx'), may hold values from -6 to 6
- helm: float32 [1024, 1024], P('gy', 'gx'), may hold values from 0.2 to 4
Outputs:
- tracer_new: float32 [8, 1024, 1024], P(None, 'gy', 'gx')
- heights: float32 [1024, 1024], P('gy', 'gx')
Inputs may be any that keep to these rules, and one draw needn't show every extreme that they name: `columns`: ocean levels per column; 0 means land.
All inputs are finite; a program needn't handle non-finite values.
Results may differ from a plain program's by a relative error of at most 0.0001.
Values sent between devices are 32-bit elements; how exact they have to be, the bound alone decides.
A program may use at most 64 MiB of HBM per device.

v0:
```python
import jax
import jax.numpy as jnp
from jax import lax
from jax.sharding import PartitionSpec as P

TSTEPS = 2
ITERS = 3


def extended_2(array, sides, width, wrap):
    for axis, dim in sides:
        peers, length = (lax.axis_size(axis), array.shape[dim])
        up = [(i, (i + 1) % peers) for i in range(peers if wrap else peers - 1)]
        down = [(j, i) for i, j in up]
        last = lax.slice_in_dim(array, length - width, length, axis=dim)
        first = lax.slice_in_dim(array, 0, width, axis=dim)
        before = lax.ppermute(last, axis, up)
        after = lax.ppermute(first, axis, down)
        array = jnp.concatenate([before, array, after], axis=dim)
    return array


def upwind(speed, behind, ahead):
    return jnp.maximum(speed, 0.0) * behind + jnp.minimum(speed, 0.0) * ahead


def advect_block(extended, east_ext, north_ext, ocean_ext):
    centre = extended[:, 1:-1, 1:-1]
    open_east = ocean_ext[:, 1:-1, :-1] * ocean_ext[:, 1:-1, 1:]
    flux_east = open_east * upwind(
        east_ext[:, 1:-1, :-1], extended[:, 1:-1, :-1], extended[:, 1:-1, 1:]
    )
    open_north = ocean_ext[:, :-1, 1:-1] * ocean_ext[:, 1:, 1:-1]
    flux_north = open_north * upwind(
        north_ext[:, :-1, 1:-1], extended[:, :-1, 1:-1], extended[:, 1:, 1:-1]
    )
    return centre - (
        flux_east[:, :, 1:] - flux_east[:, :, :-1] + flux_north[:, 1:, :] - flux_north[:, :-1, :]
    )


def stencil(extended, wet_ext, diagonal_term):
    weighted = wet_ext * extended
    edges = weighted[1:-1, 2:] + weighted[1:-1, :-2] + weighted[2:, 1:-1] + weighted[:-2, 1:-1]
    corners = weighted[2:, 2:] + weighted[2:, :-2] + weighted[:-2, 2:] + weighted[:-2, :-2]
    return diagonal_term * extended[1:-1, 1:-1] - wet_ext[1:-1, 1:-1] * (edges + 0.5 * corners)


def wrap_columns(source):
    return jnp.concatenate([source[:, -1:], source, source[:, :1]], axis=1)


def solve(forcing, diagonal_term, apply_matrix, sum_all):
    heights = jnp.zeros_like(forcing)
    residual = forcing
    scaled = residual / diagonal_term
    applied = apply_matrix(scaled)
    product_now, curvature = sum_all((jnp.sum(residual * scaled), jnp.sum(applied * scaled)))
    step_size = product_now / curvature
    direction = scaled
    along = applied
    for iteration in range(ITERS):
        heights = heights + step_size * direction
        residual = residual - step_size * along
        if iteration + 1 < ITERS:
            scaled = residual / diagonal_term
            applied = apply_matrix(scaled)
            product_next, curvature = sum_all(
                (jnp.sum(residual * scaled), jnp.sum(applied * scaled))
            )
            factor = product_next / product_now
            step_size = product_next / (curvature - factor * product_next / step_size)
            direction = scaled + factor * direction
            along = applied + factor * along
            product_now = product_next
    return heights


def on_device(tracer, east_speed, north_speed, columns, thickness, surface_flux, helm):
    levels, rows_dev, cols_dev = tracer.shape
    depth = lax.broadcasted_iota(jnp.int32, tracer.shape, 0)
    ocean = (depth < columns[None]).astype(jnp.float32)
    stacked = jnp.stack([east_speed, north_speed, ocean])
    static_ext = extended_2(stacked, (("gy", 2), ("gx", 3)), 1, True)
    position = lax.axis_index("gy")
    last_row = lax.axis_size("gy") - 1
    row_ids = lax.broadcasted_iota(jnp.int32, (rows_dev + 2, 1), 0)
    closed = (row_ids == 0) & (position == 0) | (row_ids == rows_dev + 1) & (position == last_row)
    row_keep = jnp.where(closed, 0.0, 1.0).astype(jnp.float32)
    ocean_ext = static_ext[2] * row_keep[None]
    current = tracer
    for section_index in range(TSTEPS):
        extended = extended_2(current, (("gy", 1), ("gx", 2)), 1, True)
        current = advect_block(extended, static_ext[0], static_ext[1], ocean_ext)
    forcing = surface_flux + jnp.sum(thickness[:, None, None] * ocean * current, axis=0)
    band_rhs, band_helm, band_wet = (
        lax.all_gather(forcing, "gx", axis=1, tiled=True),
        lax.all_gather(helm, "gx", axis=1, tiled=True),
        lax.all_gather(ocean_ext[0, :, 1:-1], "gx", axis=1, tiled=True),
    )
    wet_wrapped = wrap_columns(band_wet)
    band_diagonal = 6.0 + band_helm

    def apply_band(source):
        rimmed = extended_2(source, (("gy", 0),), 1, False)
        return stencil(wrap_columns(rimmed), wet_wrapped, band_diagonal)

    def sum_band(values):
        return lax.psum(values, "gy")

    band_heights = solve(band_rhs, band_diagonal, apply_band, sum_band)
    heights = lax.dynamic_slice_in_dim(band_heights, lax.axis_index("gx") * cols_dev, cols_dev, 1)
    return (current, heights)


def solution(mesh):
    in_specs = (
        P(None, "gy", "gx"),
        P(None, "gy", "gx"),
        P(None, "gy", "gx"),
        P("gy", "gx"),
        P(),
        P("gy", "gx"),
        P("gy", "gx"),
    )
    out_specs = (P(None, "gy", "gx"), P("gy", "gx"))
    return jax.shard_map(
        on_device, mesh=mesh, in_specs=in_specs, out_specs=out_specs, check_vma=False
    )
```

profile of v0, /device:TPU:4, one launch (start us, length us, event | category | flops | bytes accessed | tf_op | source)
XLA Modules:
  0.0 213.6 jit_solution(6373276697639543300)
XLA Ops:
  3.0 2.6 %collective-permute-start.1 = (f32[3,8,1,256]{3,2,1,0:T(1,128)S(1)}, f32[3,8,1,256]{3,2,1,0:T(1,128)S(1)}, u32[]{:S(2)}, u32[]{:S(2)}) collective-permute-start(f32[3,8,1,256]{3,2,1,0:T(1,128)S(1)} %get-tuple-element.27), channel_id=1, source_target_pairs={{4,0},{8,4},{12,8},{16,12},{20,16},{24,20},{28,24},{0,28},{5,1},{9... | collective-permute-start | bytes 73736 | tf_op jit(solution)/shard_map/ppermute | solution.py:18
  5.7 2.6 %collective-permute-start.5 = (f32[8,1,256]{2,1,0:T(1,128)S(1)}, f32[8,1,256]{2,1,0:T(1,128)S(1)}, u32[]{:S(2)}, u32[]{:S(2)}) collective-permute-start(f32[8,1,256]{2,1,0:T(1,128)S(1)} %get-tuple-element.34), channel_id=1, source_target_pairs={{4,0},{8,4},{12,8},{16,12},{20,16},{24,20},{28,24},{0,28},{5,1},{9... | collective-permute-start | bytes 24584 | tf_op jit(solution)/shard_map/ppermute | solution.py:18
  8.3 15.8 %all_gather.10 = f32[128,1024]{1,0:T(8,128)S(1)} all-gather(f32[128,256]{1,0:T(8,128)S(1)} %copy-done.16), channel_id=1, replica_groups=mesh['gy'=8,'gx'=4] {'gx'}, dimensions={1}, use_global_device_ids=true | all-gather | bytes 655360 | tf_op jit(solution)/shard_map/all_gather | solution.py:98
  27.8 3.1 %collective-permute-start.7 = (f32[8,130,1]{1,0,2:T(8,128)S(1)}, f32[8,130,1]{1,0,2:T(8,128)S(1)}, u32[]{:S(2)}, u32[]{:S(2)}) collective-permute-start(f32[8,130,1]{1,0,2:T(8,128)S(1)} %copy.29), channel_id=1, source_target_pairs={{1,0},{2,1},{3,2},{0,3},{5,4},{6,5},{7,6},{4,7},{9,8},{10,9},{11,1... | collective-permute-start | bytes 12488 | tf_op jit(solution)/shard_map/ppermute | solution.py:18
  30.9 1.9 pad_maximum_fusion.1
  32.8 2.2 %fusion.35 = (f32[3,8,130,1]{3,2,1,0:T(8,128)}, f32[3,8,130,1]{3,2,1,0:T(8,128)}) fusion(f32[3,8,130,256]{3,2,1,0:T(8,128)S(1)} %pad_maximum_fusion.1), kind=kLoop, calls=%fused_computation.108 | loop fusion | bytes 49920 | tf_op jit(solution)/shard_map/slice | solution.py:15
  35.0 2.3 %copy.23 = f32[3,8,130,1]{2,1,3,0:T(8,128)S(1)} copy(f32[3,8,130,1]{3,2,1,0:T(8,128)} %get-tuple-element.24) | data formatting | bytes 24960 | tf_op jit(solution)/shard_map/slice | solution.py:15
  37.4 2.3 %copy.24 = f32[3,8,130,1]{2,1,3,0:T(8,128)S(1)} copy(f32[3,8,130,1]{3,2,1,0:T(8,128)} %get-tuple-element.25) | data formatting | bytes 24960 | tf_op jit(solution)/shard_map/slice | solution.py:16
  39.7 3.8 %collective-permute-start.3 = (f32[3,8,130,1]{2,1,3,0:T(8,128)S(1)}, f32[3,8,130,1]{2,1,3,0:T(8,128)S(1)}, u32[]{:S(2)}, u32[]{:S(2)}) collective-permute-start(f32[3,8,130,1]{2,1,3,0:T(8,128)S(1)} %copy.24), channel_id=1, source_target_pairs={{1,0},{2,1},{3,2},{0,3},{5,4},{6,5},{7,6},{4,7},{9,8},{10,9},{11,1... | collective-permute-start | bytes 37448 | tf_op jit(solution)/shard_map/ppermute | solution.py:18
  45.7 1.8 copy.25
  47.5 1.8 copy.26
  49.3 5.7 %pad_maximum_fusion = f32[3,8,130,258]{3,2,1,0:T(8,128)S(1)} fusion(f32[3,8,130,1]{3,2,1,0:T(8,128)} %copy.26, f32[3,8,1,256]{3,2,1,0:T(1,128)S(1)} %collective-permute-done.1, f32[1,8,128,256]{3,2,1,0:T(8,128)S(1)} %fusion.15, f32[1,8,128,256]{3,2,1,0:T(8,128)} %bitcast.24, f32[1,8,128,256]{3,2,1,0:T(8,128)} %bitcast.28, ...), kind=kLoop, calls=%fused_computation | loop fusion | flops 4829760 | bytes 6439680 | tf_op jit(solution)/shard_map/concatenate | solution.py:19
  59.3 2.6 %collective-permute-start.9 = (f32[8,1,256]{2,1,0:T(1,128)S(1)}, f32[8,1,256]{2,1,0:T(1,128)S(1)}, u32[]{:S(2)}, u32[]{:S(2)}) collective-permute-start(f32[8,1,256]{2,1,0:T(1,128)S(1)} %get-tuple-element.32), channel_id=1, source_target_pairs={{4,0},{8,4},{12,8},{16,12},{20,16},{24,20},{28,24},{0,28},{5,1},{9... | collective-permute-start | bytes 24584 | tf_op jit(solution)/shard_map/ppermute | solution.py:18
  62.0 16.8 %all-gather = f32[1,130,1024]{2,1,0:T(8,128)} all-gather(f32[1,130,256]{2,1,0:T(8,128)S(1)} %slice.340), channel_id=2, replica_groups=mesh['gy'=8,'gx'=4] {'gx'}, dimensions={2}, use_global_device_ids=true | all-gather | bytes 665600 | tf_op jit(solution)/shard_map/all_gather | solution.py:99
  82.9 4.0 %collective-permute-start.11 = (f32[8,130,1]{1,0,2:T(8,128)S(1)}, f32[8,130,1]{1,0,2:T(8,128)S(1)}, u32[]{:S(2)}, u32[]{:S(2)}) collective-permute-start(f32[8,130,1]{1,0,2:T(8,128)S(1)} %copy.33), channel_id=1, source_target_pairs={{1,0},{2,1},{3,2},{0,3},{5,4},{6,5},{7,6},{4,7},{9,8},{10,9},{11,1... | collective-permute-start | bytes 12488 | tf_op jit(solution)/shard_map/ppermute | solution.py:18
  86.9 3.4 %fusion.12 = f32[8,129,256]{2,1,0:T(8,128)} fusion(f32[8,128,256]{2,1,0:T(8,128)S(1)} %fusion.14, f32[8,1,256]{2,1,0:T(1,128)S(1)} %collective-permute-done.8, f32[8,1,256]{2,1,0:T(1,128)S(1)} %collective-permute-done.9, f32[8,130,258]{2,1,0:T(8,128)} %copy-done.6, f32[8,130,258]{2,1,0:T(8,128)S(1)} %fusion), kind=kLoop, calls=%fused_computation.38 | loop fusion | flops 2377728 | bytes 5292032 | tf_op jit(solution)/shard_map/mul | solution.py:34
  92.4 3.0 %fusion.3 = f32[8,128,257]{2,1,0:T(8,128)S(1)} fusion(f32[8,130,1]{2,1,0:T(8,128)} %copy.34, f32[8,1,256]{2,1,0:T(1,128)S(1)} %collective-permute-done.9, f32[8,128,256]{2,1,0:T(8,128)S(1)} %fusion.14, f32[8,1,256]{2,1,0:T(1,128)S(1)} %collective-permute-done.8, f32[8,130,1]{2,1,0:T(8,128)} %copy.32, f32[8,130,258]{2,1,0:T(8,128)} %copy-done.3, ...), kind=kLoop, calls=%fused_computation.9 | loop fusion | flops 3421184 | bytes 5283968 | tf_op jit(solution)/shard_map/mul | solution.py:30
  96.9 15.9 %all_gather.9 = f32[128,1024]{1,0:T(8,128)S(1)} all-gather(f32[128,256]{1,0:T(8,128)S(1)} %add.126), channel_id=1, replica_groups=mesh['gy'=8,'gx'=4] {'gx'}, dimensions={1}, use_global_device_ids=true | all-gather | bytes 655360 | tf_op jit(solution)/shard_map/all_gather | solution.py:97
  113.0 1.9 collective-permute-start.12
  114.9 4.5 %collective-permute-start.13 = (f32[1,1024]{1,0:T(1,128)S(1)}, f32[1,1024]{1,0:T(1,128)S(1)}, u32[]{:S(2)}, u32[]{:S(2)}) collective-permute-start(f32[1,1024]{1,0:T(1,128)S(1)} %get-tuple-element.49), channel_id=1, source_target_pairs={{4,0},{8,4},{12,8},{16,12},{20,16},{24,20},{28,24},{5,1},{9,5},{13... | collective-permute-start | bytes 12296 | tf_op jit(solution)/shard_map/ppermute | solution.py:18
  121.7 2.1 %concatenate.73 = f32[130,1026]{1,0:T(8,128)} concatenate(f32[130,1]{1,0:T(8,128)S(1)} %get-tuple-element.41, f32[130,1024]{1,0:T(8,128)} %copy-done.9, f32[130,1]{1,0:T(8,128)S(1)} %get-tuple-element.40), dimensions={1} | concatenate | bytes 1067040 | tf_op jit(solution)/shard_map/concatenate | solution.py:50
  126.4 15.1 %all-reduce.2 = (f32[]{:T(128)}, f32[]{:T(128)}) all-reduce(f32[]{:T(128)} %get-tuple-element.9, f32[]{:T(128)} %get-tuple-element.8), channel_id=1, replica_groups=mesh['gy'=8,'gx'=4] {'gy'}, use_global_device_ids=true, to_apply=%region_2.3 | all-reduce | flops 2 | bytes 16 | tf_op jit(solution)/shard_map/psum | solution.py:109
  143.1 1.9 collective-permute-start.14
  145.0 4.5 %collective-permute-start.15 = (f32[1,1024]{1,0:T(1,128)S(1)}, f32[1,1024]{1,0:T(1,128)S(1)}, u32[]{:S(2)}, u32[]{:S(2)}) collective-permute-start(f32[1,1024]{1,0:T(1,128)S(1)} %get-tuple-element.47), channel_id=1, source_target_pairs={{4,0},{8,4},{12,8},{16,12},{20,16},{24,20},{28,24},{5,1},{9,5},{13... | collective-permute-start | bytes 12296 | tf_op jit(solution)/shard_map/ppermute | solution.py:18
  151.8 2.1 %concatenate.75 = f32[130,1026]{1,0:T(8,128)} concatenate(f32[130,1]{1,0:T(8,128)S(1)} %get-tuple-element.39, f32[130,1024]{1,0:T(8,128)} %copy-done.10, f32[130,1]{1,0:T(8,128)S(1)} %get-tuple-element.38), dimensions={1} | concatenate | bytes 1067040 | tf_op jit(solution)/shard_map/concatenate | solution.py:50
  155.2 2.2 %multiply_reduce_fusion.2 = (f32[]{:T(128)}, f32[]{:T(128)}, f32[128,1024]{1,0:T(8,128)}) fusion(f32[128,1024]{1,0:T(8,128)S(1)} %copy-done.8, f32[128,1024]{1,0:T(8,128)S(1)} %all_gather.9, f32[128,1024]{1,0:T(8,128)S(1)} %get-tuple-element.19, f32[]{:T(128)S(6)} %div.31, f32[130,1026]{1,0:T(8,128)S(1)} %mul.198, f32[1,130,1024]{2,1,0:T(8,128)S(1)} %copy-done.2, ...), kind=kLoop, calls=%fused_computation.92 | loop fusion | flops 2359294 | bytes 7340044 | tf_op jit(solution)/shard_map/reduce_sum | solution.py:69
  157.4 15.1 %all-reduce.1 = (f32[]{:T(128)}, f32[]{:T(128)}) all-reduce(f32[]{:T(128)} %get-tuple-element.7, f32[]{:T(128)} %get-tuple-element.6), channel_id=1, replica_groups=mesh['gy'=8,'gx'=4] {'gy'}, use_global_device_ids=true, to_apply=%region_6.7 | all-reduce | flops 2 | bytes 16 | tf_op jit(solution)/shard_map/psum | solution.py:109
  177.3 2.1 add_divide_fusion
  180.2 1.9 collective-permute-start.16
  182.1 4.5 %collective-permute-start.17 = (f32[1,1024]{1,0:T(1,128)S(1)}, f32[1,1024]{1,0:T(1,128)S(1)}, u32[]{:S(2)}, u32[]{:S(2)}) collective-permute-start(f32[1,1024]{1,0:T(1,128)S(1)} %get-tuple-element.45), channel_id=1, source_target_pairs={{4,0},{8,4},{12,8},{16,12},{20,16},{24,20},{28,24},{5,1},{9,5},{13... | collective-permute-start | bytes 12296 | tf_op jit(solution)/shard_map/ppermute | solution.py:18
  192.9 15.0 %all-reduce = (f32[]{:T(128)}, f32[]{:T(128)}) all-reduce(f32[]{:T(128)} %get-tuple-element.5, f32[]{:T(128)} %get-tuple-element.4), channel_id=1, replica_groups=mesh['gy'=8,'gx'=4] {'gy'}, use_global_device_ids=true, to_apply=%region_10.11 | all-reduce | flops 2 | bytes 16 | tf_op jit(solution)/shard_map/psum | solution.py:109
  211.9 1.7 fusion.31
  (106 shorter events, 35.7 us)
Async XLA Ops:
  0.6 1.3 copy-start.4
  1.9 3.7 %copy-start = (f32[8,128,256]{2,1,0:T(8,128)S(1)}, f32[8,128,256]{2,1,0:T(8,128)}, u32[]{:S(2)}) copy-start(f32[8,128,256]{2,1,0:T(8,128)} %param.7) | copy-start | bytes 3145732
  1.9 6.4 %copy-start.16 = (f32[128,256]{1,0:T(8,128)S(1)}, f32[128,256]{1,0:T(8,128)}, u32[]{:S(2)}) copy-start(f32[128,256]{1,0:T(8,128)} %param.13) | copy-start | bytes 393220
  2.9 28.0 %collective-permute-start = (f32[3,8,1,256]{3,2,1,0:T(1,128)S(1)}, f32[3,8,1,256]{3,2,1,0:T(1,128)S(1)}, u32[]{:S(2)}, u32[]{:S(2)}) collective-permute-start(f32[3,8,1,256]{3,2,1,0:T(1,128)S(1)} %get-tuple-element.26), channel_id=1, source_target_pairs={{0,4},{4,8},{8,12},{12,16},{16,20},{20,24},{24,28},{28,0},{1,5},{5... | collective-permute-start | bytes 73736 | tf_op jit(solution)/shard_map/ppermute | solution.py:17
  3.0 27.9 %collective-permute-start.1 = (f32[3,8,1,256]{3,2,1,0:T(1,128)S(1)}, f32[3,8,1,256]{3,2,1,0:T(1,128)S(1)}, u32[]{:S(2)}, u32[]{:S(2)}) collective-permute-start(f32[3,8,1,256]{3,2,1,0:T(1,128)S(1)} %get-tuple-element.27), channel_id=1, source_target_pairs={{4,0},{8,4},{12,8},{16,12},{20,16},{24,20},{28,24},{0,28},{5,1},{9... | collective-permute-start | bytes 73736 | tf_op jit(solution)/shard_map/ppermute | solution.py:18
  5.6 18.5 %collective-permute-start.4 = (f32[8,1,256]{2,1,0:T(1,128)S(1)}, f32[8,1,256]{2,1,0:T(1,128)S(1)}, u32[]{:S(2)}, u32[]{:S(2)}) collective-permute-start(f32[8,1,256]{2,1,0:T(1,128)S(1)} %get-tuple-element.35), channel_id=1, source_target_pairs={{0,4},{4,8},{8,12},{12,16},{16,20},{20,24},{24,28},{28,0},{1,5},{5... | collective-permute-start | bytes 24584 | tf_op jit(solution)/shard_map/ppermute | solution.py:17
  5.7 18.5 %collective-permute-start.5 = (f32[8,1,256]{2,1,0:T(1,128)S(1)}, f32[8,1,256]{2,1,0:T(1,128)S(1)}, u32[]{:S(2)}, u32[]{:S(2)}) collective-permute-start(f32[8,1,256]{2,1,0:T(1,128)S(1)} %get-tuple-element.34), channel_id=1, source_target_pairs={{4,0},{8,4},{12,8},{16,12},{20,16},{24,20},{28,24},{0,28},{5,1},{9... | collective-permute-start | bytes 24584 | tf_op jit(solution)/shard_map/ppermute | solution.py:18
  26.7 16.8 %collective-permute-start.6 = (f32[8,130,1]{1,0,2:T(8,128)S(1)}, f32[8,130,1]{1,0,2:T(8,128)S(1)}, u32[]{:S(2)}, u32[]{:S(2)}) collective-permute-start(f32[8,130,1]{1,0,2:T(8,128)S(1)} %copy.27), channel_id=1, source_target_pairs={{0,1},{1,2},{2,3},{3,0},{4,5},{5,6},{6,7},{7,4},{8,9},{9,10},{10,1... | collective-permute-start | bytes 12488 | tf_op jit(solution)/shard_map/ppermute | solution.py:17
  27.8 16.8 %collective-permute-start.7 = (f32[8,130,1]{1,0,2:T(8,128)S(1)}, f32[8,130,1]{1,0,2:T(8,128)S(1)}, u32[]{:S(2)}, u32[]{:S(2)}) collective-permute-start(f32[8,130,1]{1,0,2:T(8,128)S(1)} %copy.29), channel_id=1, source_target_pairs={{1,0},{2,1},{3,2},{0,3},{5,4},{6,5},{7,6},{4,7},{9,8},{10,9},{11,1... | collective-permute-start | bytes 12488 | tf_op jit(solution)/shard_map/ppermute | solution.py:18
  37.3 8.3 %collective-permute-start.2 = (f32[3,8,130,1]{2,1,3,0:T(8,128)S(1)}, f32[3,8,130,1]{2,1,3,0:T(8,128)S(1)}, u32[]{:S(2)}, u32[]{:S(2)}) collective-permute-start(f32[3,8,130,1]{2,1,3,0:T(8,128)S(1)} %copy.23), channel_id=1, source_target_pairs={{0,1},{1,2},{2,3},{3,0},{4,5},{5,6},{6,7},{7,4},{8,9},{9,10},{10,1... | collective-permute-start | bytes 37448 | tf_op jit(solution)/shard_map/ppermute | solution.py:17
  39.7 7.8 %collective-permute-start.3 = (f32[3,8,130,1]{2,1,3,0:T(8,128)S(1)}, f32[3,8,130,1]{2,1,3,0:T(8,128)S(1)}, u32[]{:S(2)}, u32[]{:S(2)}) collective-permute-start(f32[3,8,130,1]{2,1,3,0:T(8,128)S(1)} %copy.24), channel_id=1, source_target_pairs={{1,0},{2,1},{3,2},{0,3},{5,4},{6,5},{7,6},{4,7},{9,8},{10,9},{11,1... | collective-permute-start | bytes 37448 | tf_op jit(solution)/shard_map/ppermute | solution.py:18
  55.2 2.2 %copy-start.3 = (f32[8,130,258]{2,1,0:T(8,128)}, f32[8,130,258]{2,1,0:T(8,128)S(1)}, u32[]{:S(2)}) copy-start(f32[8,130,258]{2,1,0:T(8,128)S(1)} %get-tuple-element.22) | copy-start | bytes 3219844
  56.4 1.2 copy-start.13
  57.6 1.3 copy-start.1
  59.3 19.5 %collective-permute-start.8 = (f32[8,1,256]{2,1,0:T(1,128)S(1)}, f32[8,1,256]{2,1,0:T(1,128)S(1)}, u32[]{:S(2)}, u32[]{:S(2)}) collective-permute-start(f32[8,1,256]{2,1,0:T(1,128)S(1)} %get-tuple-element.33), channel_id=1, source_target_pairs={{0,4},{4,8},{8,12},{12,16},{16,20},{20,24},{24,28},{28,0},{1,5},{5... | collective-permute-start | bytes 24584 | tf_op jit(solution)/shard_map/ppermute | solution.py:17
  59.3 19.5 %collective-permute-start.9 = (f32[8,1,256]{2,1,0:T(1,128)S(1)}, f32[8,1,256]{2,1,0:T(1,128)S(1)}, u32[]{:S(2)}, u32[]{:S(2)}) collective-permute-start(f32[8,1,256]{2,1,0:T(1,128)S(1)} %get-tuple-element.32), channel_id=1, source_target_pairs={{4,0},{8,4},{12,8},{16,12},{20,16},{24,20},{28,24},{0,28},{5,1},{9... | collective-permute-start | bytes 24584 | tf_op jit(solution)/shard_map/ppermute | solution.py:18
  81.5 8.8 %collective-permute-start.10 = (f32[8,130,1]{1,0,2:T(8,128)S(1)}, f32[8,130,1]{1,0,2:T(8,128)S(1)}, u32[]{:S(2)}, u32[]{:S(2)}) collective-permute-start(f32[8,130,1]{1,0,2:T(8,128)S(1)} %copy.31), channel_id=1, source_target_pairs={{0,1},{1,2},{2,3},{3,0},{4,5},{5,6},{6,7},{7,4},{8,9},{9,10},{10,1... | collective-permute-start | bytes 12488 | tf_op jit(solution)/shard_map/ppermute | solution.py:17
  82.9 8.4 %collective-permute-start.11 = (f32[8,130,1]{1,0,2:T(8,128)S(1)}, f32[8,130,1]{1,0,2:T(8,128)S(1)}, u32[]{:S(2)}, u32[]{:S(2)}) collective-permute-start(f32[8,130,1]{1,0,2:T(8,128)S(1)} %copy.33), channel_id=1, source_target_pairs={{1,0},{2,1},{3,2},{0,3},{5,4},{6,5},{7,6},{4,7},{9,8},{10,9},{11,1... | collective-permute-start | bytes 12488 | tf_op jit(solution)/shard_map/ppermute | solution.py:18
  92.4 3.0 %copy-start.5 = (f32[8,129,256]{2,1,0:T(8,128)S(1)}, f32[8,129,256]{2,1,0:T(8,128)}, u32[]{:S(2)}) copy-start(f32[8,129,256]{2,1,0:T(8,128)} %fusion.12) | copy-start | bytes 3170308
  92.4 3.0 %copy-start.15 = (s32[128,256]{1,0:T(8,128)S(1)}, s32[128,256]{1,0:T(8,128)}, u32[]{:S(2)}) copy-start(s32[128,256]{1,0:T(8,128)} %param.10) | copy-start | bytes 393220
  92.4 3.0 %copy-start.18 = (f32[8]{0:T(128)S(1)}, f32[8]{0:T(128)}, u32[]{:S(2)}) copy-start(f32[8]{0:T(128)} %param.11) | copy-start | bytes 100
  95.4 1.5 copy-start.17
  96.9 22.6 %copy-start.2 = (f32[1,130,1024]{2,1,0:T(8,128)S(1)}, f32[1,130,1024]{2,1,0:T(8,128)}, u32[]{:S(2)}) copy-start(f32[1,130,1024]{2,1,0:T(8,128)} %all-gather) | copy-start | bytes 1597444
  113.0 6.9 %collective-permute-start.12 = (f32[1,1024]{1,0:T(1,128)S(1)}, f32[1,1024]{1,0:T(1,128)S(1)}, u32[]{:S(2)}, u32[]{:S(2)}) collective-permute-start(f32[1,1024]{1,0:T(1,128)S(1)} %get-tuple-element.48), channel_id=1, source_target_pairs={{0,4},{4,8},{8,12},{12,16},{16,20},{20,24},{24,28},{1,5},{5,9},{9,... | collective-permute-start | bytes 12296 | tf_op jit(solution)/shard_map/ppermute | solution.py:17
  114.9 5.9 %collective-permute-start.13 = (f32[1,1024]{1,0:T(1,128)S(1)}, f32[1,1024]{1,0:T(1,128)S(1)}, u32[]{:S(2)}, u32[]{:S(2)}) collective-permute-start(f32[1,1024]{1,0:T(1,128)S(1)} %get-tuple-element.49), channel_id=1, source_target_pairs={{4,0},{8,4},{12,8},{16,12},{20,16},{24,20},{28,24},{5,1},{9,5},{13... | collective-permute-start | bytes 12296 | tf_op jit(solution)/shard_map/ppermute | solution.py:18
  143.0 7.8 %copy-start.7 = (f32[128,1024]{1,0:T(8,128)}, f32[128,1024]{1,0:T(8,128)S(1)}, u32[]{:S(2)}) copy-start(f32[128,1024]{1,0:T(8,128)S(1)} %add_divide_fusion.1) | copy-start | bytes 1572868
  143.1 6.5 %collective-permute-start.14 = (f32[1,1024]{1,0:T(1,128)S(1)}, f32[1,1024]{1,0:T(1,128)S(1)}, u32[]{:S(2)}, u32[]{:S(2)}) collective-permute-start(f32[1,1024]{1,0:T(1,128)S(1)} %get-tuple-element.46), channel_id=1, source_target_pairs={{0,4},{4,8},{8,12},{12,16},{16,20},{20,24},{24,28},{1,5},{5,9},{9,... | collective-permute-start | bytes 12296 | tf_op jit(solution)/shard_map/ppermute | solution.py:17
  145.0 5.9 %collective-permute-start.15 = (f32[1,1024]{1,0:T(1,128)S(1)}, f32[1,1024]{1,0:T(1,128)S(1)}, u32[]{:S(2)}, u32[]{:S(2)}) collective-permute-start(f32[1,1024]{1,0:T(1,128)S(1)} %get-tuple-element.47), channel_id=1, source_target_pairs={{4,0},{8,4},{12,8},{16,12},{20,16},{24,20},{28,24},{5,1},{9,5},{13... | collective-permute-start | bytes 12296 | tf_op jit(solution)/shard_map/ppermute | solution.py:18
  153.9 1.2 copy-start.8
  180.2 6.5 %collective-permute-start.16 = (f32[1,1024]{1,0:T(1,128)S(1)}, f32[1,1024]{1,0:T(1,128)S(1)}, u32[]{:S(2)}, u32[]{:S(2)}) collective-permute-start(f32[1,1024]{1,0:T(1,128)S(1)} %get-tuple-element.44), channel_id=1, source_target_pairs={{0,4},{4,8},{8,12},{12,16},{16,20},{20,24},{24,28},{1,5},{5,9},{9,... | collective-permute-start | bytes 12296 | tf_op jit(solution)/shard_map/ppermute | solution.py:17
  182.1 5.9 %collective-permute-start.17 = (f32[1,1024]{1,0:T(1,128)S(1)}, f32[1,1024]{1,0:T(1,128)S(1)}, u32[]{:S(2)}, u32[]{:S(2)}) collective-permute-start(f32[1,1024]{1,0:T(1,128)S(1)} %get-tuple-element.45), channel_id=1, source_target_pairs={{4,0},{8,4},{12,8},{16,12},{20,16},{24,20},{28,24},{5,1},{9,5},{13... | collective-permute-start | bytes 12296 | tf_op jit(solution)/shard_map/ppermute | solution.py:18
  190.3 1.2 copy-start.14
  (5 other events, 4.7 us)
where the time goes:
time: 215 us; the launch traced here: 214 us
  blocking collectives  93.8 us (44%)
  starting transfers between devices  39.2 us (18%)
  other arithmetic  34.3 us (16%)
  local copies, waits for them, and re-layouts  31.6 us (15%)
  between operations  11.2 us (5%)
  waiting for transfers between devices  3.47 us (2%)
    psum x3, blocking collectives, sum_band(): return lax.psum(values, 'gy')  45.2 us
    ppermute x9, starting transfers between devices, extended_2(): after = lax.ppermute(first, axis, down)  32.5 us
    all_gather x1, blocking collectives, on_device(): lax.all_gather(ocean_ext[0, :, 1:-1], 'gx', axis=1, tiled=True)  16.8 us
    all_gather x1, blocking collectives, on_device(): lax.all_gather(forcing, 'gx', axis=1, tiled=True)  15.9 us
    all_gather x1, blocking collectives, on_device(): lax.all_gather(helm, 'gx', axis=1, tiled=True)  15.8 us
    slice x9, local copies, waits for them, and re-layouts, extended_2(): last = lax.slice_in_dim(array, length - width, length, axis=dim)  9.51 us
    concatenate x7, other arithmetic, extended_2(): array = jnp.concatenate([before, array, after], axis=dim)  8.97 us
    ppermute x9, starting transfers between devices, extended_2(): before = lax.ppermute(last, axis, up)  6.72 us
  transfers between devices with their start and end apart: 18, of which 3 were waited for; matrix products, arithmetic and copies ran while one was open for 10% of the time, Pallas kernels for 0%

commit v1 on v0

--- a/solution.py
+++ b/solution.py
@@ -96,7 +96,7 @@
     band_rhs, band_helm, band_wet = (
         lax.all_gather(forcing, "gx", axis=1, tiled=True),
         lax.all_gather(helm, "gx", axis=1, tiled=True),
-        lax.all_gather(ocean_ext[0, :, 1:-1], "gx", axis=1, tiled=True),
+        jnp.concatenate(lax.all_gather(ocean_ext[0, :, 1:-1], "gx"), axis=1),
     )
     wet_wrapped = wrap_columns(band_wet)
     band_diagonal = 6.0 + band_helm

time: 215 us -> 223 us (1.037)
  local copies, waits for them, and re-layouts: 31.6 us -> 49.5 us
  blocking collectives: 93.8 us -> 88.6 us
  other arithmetic: 34.3 us -> 32 us
    unnamed x38 -> x58, local copies, waits for them, and re-layouts: 3.82 us -> 14.8 us
    psum x3, blocking collectives: 45.2 us -> 41.9 us  [sum_band(): return lax.psum(values, 'gy')]
    another operation x0 -> x1, local copies, waits for them, and re-layouts: none -> 2.44 us  [on_device(): stacked = jnp.stack([east_speed, north_speed, ocean])]
    concatenate x7 -> x6, other arithmetic: 8.97 us -> 7.59 us  [extended_2(): array = jnp.concatenate([before, array, after], axis=dim)]
  transfers between devices with their start and end apart: 18 -> 18, of which waited for: 3 -> 1; matrix products, arithmetic and copies ran while one was open for 10% -> 14% of each run, Pallas kernels for 0% -> 0%
where the time goes in v1:
time: 223 us; the launch traced here: 221 us
  blocking collectives  88.6 us (40%)
  local copies, waits for them, and re-layouts  49.5 us (22%)
  starting transfers between devices  38.9 us (17%)
  other arithmetic  32 us (14%)
  between operations  10.9 us (5%)
    psum x3, blocking collectives, sum_band(): return lax.psum(values, 'gy')  41.9 us
    ppermute x9, starting transfers between devices, extended_2(): after = lax.ppermute(first, axis, down)  30.4 us
    all_gather x1, blocking collectives, on_device(): lax.all_gather(ocean_ext[0, :, 1:-1], 'gx')  16.1 us
    all_gather x1, blocking collectives, on_device(): lax.all_gather(forcing, 'gx', axis=1, tiled=True)  15.7 us
    all_gather x1, blocking collectives, on_device(): lax.all_gather(helm, 'gx', axis=1, tiled=True)  15 us
    unnamed x58, local copies, waits for them, and re-layouts  14.8 us
    slice x9, local copies, waits for them, and re-layouts, extended_2(): last = lax.slice_in_dim(array, length - width, length, axis=dim)  9.44 us
    ppermute x9, starting transfers between devices, extended_2(): before = lax.ppermute(last, axis, up)  8.53 us
  transfers between devices with their start and end apart: 18, of which 1 were waited for; matrix products, arithmetic and copies ran while one was open for 14% of the time, Pallas kernels for 0%

profile of v1, /device:TPU:4, one launch (start us, length us, event | category | flops | bytes accessed | tf_op | source)
XLA Modules:
  0.0 221.3 jit_solution(2328757100309373554)
XLA Ops:
  1.9 2.4 %copy_bitcast_fusion = (f32[1,8,128,256]{3,1,2,0:T(8,128)S(1)}, f32[1,8,128,256]{3,1,2,0:T(8,128)S(1)}) fusion(f32[8,128,256]{2,1,0:T(8,128)S(1)} %copy-done.21, f32[8,128,256]{2,1,0:T(8,128)} %param.8), kind=kLoop, calls=%fused_computation.43 | loop fusion | bytes 4194304 | tf_op jit(solution)/shard_map/stack | solution.py:83
  5.4 2.6 %collective-permute-start.1 = (f32[3,8,1,256]{3,1,2,0:T(8,128)S(1)}, f32[3,8,1,256]{3,1,2,0:T(8,128)S(1)}, u32[]{:S(2)}, u32[]{:S(2)}) collective-permute-start(f32[3,8,1,256]{3,1,2,0:T(8,128)S(1)} %get-tuple-element.33), channel_id=1, source_target_pairs={{4,0},{8,4},{12,8},{16,12},{20,16},{24,20},{28,24},{0,28},{5,1},{9... | collective-permute-start | bytes 73736 | tf_op jit(solution)/shard_map/ppermute | solution.py:18
  11.4 15.0 %all_gather.10 = f32[128,1024]{1,0:T(8,128)S(1)} all-gather(f32[128,256]{1,0:T(8,128)S(1)} %copy-done.23), channel_id=1, replica_groups=mesh['gy'=8,'gx'=4] {'gx'}, dimensions={1}, use_global_device_ids=true | all-gather | bytes 655360 | tf_op jit(solution)/shard_map/all_gather | solution.py:98
  31.6 2.1 collective-permute-start.6
  34.1 2.0 collective-permute-start.7
  37.6 2.1 fusion.35
  39.7 2.4 %copy.75 = f32[3,8,130,1]{2,1,3,0:T(8,128)S(1)} copy(f32[3,8,130,1]{3,1,2,0:T(8,128)} %get-tuple-element.30) | data formatting | bytes 24960 | tf_op jit(solution)/shard_map/slice | solution.py:15
  42.1 2.4 %copy.76 = f32[3,8,130,1]{2,1,3,0:T(8,128)S(1)} copy(f32[3,8,130,1]{3,1,2,0:T(8,128)} %get-tuple-element.31) | data formatting | bytes 24960 | tf_op jit(solution)/shard_map/slice | solution.py:16
  44.5 4.0 %collective-permute-start.3 = (f32[3,8,130,1]{2,1,3,0:T(8,128)S(1)}, f32[3,8,130,1]{2,1,3,0:T(8,128)S(1)}, u32[]{:S(2)}, u32[]{:S(2)}) collective-permute-start(f32[3,8,130,1]{2,1,3,0:T(8,128)S(1)} %copy.76), channel_id=1, source_target_pairs={{1,0},{2,1},{3,2},{0,3},{5,4},{6,5},{7,6},{4,7},{9,8},{10,9},{11,1... | collective-permute-start | bytes 37448 | tf_op jit(solution)/shard_map/ppermute | solution.py:18
  50.1 2.1 copy.77
  52.2 2.1 copy.78
  54.3 5.9 %pad_maximum_fusion = f32[3,8,130,258]{3,1,2,0:T(8,128)S(1)} fusion(f32[3,8,130,1]{3,1,2,0:T(8,128)} %copy.78, f32[3,8,1,256]{3,1,2,0:T(8,128)S(1)} %collective-permute-done.1, f32[1,8,128,256]{3,1,2,0:T(8,128)S(1)} %fusion.15, f32[1,8,128,256]{3,1,2,0:T(8,128)S(1)} %get-tuple-element.56, f32[1,8,128,256]{3,1,2,0:T(8,128)} %copy-done, ...), kind=kLoop, calls=%fused_computation | loop fusion | flops 4829760 | bytes 6439680 | tf_op jit(solution)/shard_map/concatenate | solution.py:19
  66.4 2.6 %collective-permute-start.9 = (f32[8,1,256]{2,0,1:T(8,128)S(1)}, f32[8,1,256]{2,0,1:T(8,128)S(1)}, u32[]{:S(2)}, u32[]{:S(2)}) collective-permute-start(f32[8,1,256]{2,0,1:T(8,128)S(1)} %get-tuple-element.38), channel_id=1, source_target_pairs={{4,0},{8,4},{12,8},{16,12},{20,16},{24,20},{28,24},{0,28},{5,1},{9... | collective-permute-start | bytes 24584 | tf_op jit(solution)/shard_map/ppermute | solution.py:18
  69.0 16.1 %all_gather.11 = f32[4,130,256]{2,1,0:T(8,128)S(1)} all-gather(f32[1,130,256]{2,1,0:T(8,128)S(1)} %copy.93), channel_id=1, replica_groups=mesh['gy'=8,'gx'=4] {'gx'}, dimensions={0}, use_global_device_ids=true | all-gather | bytes 665600 | tf_op jit(solution)/shard_map/all_gather | solution.py:99
  90.7 3.5 %collective-permute-start.11 = (f32[8,130,1]{1,0,2:T(8,128)S(1)}, f32[8,130,1]{1,0,2:T(8,128)S(1)}, u32[]{:S(2)}, u32[]{:S(2)}) collective-permute-start(f32[8,130,1]{1,0,2:T(8,128)S(1)} %copy.91), channel_id=1, source_target_pairs={{1,0},{2,1},{3,2},{0,3},{5,4},{6,5},{7,6},{4,7},{9,8},{10,9},{11,1... | collective-permute-start | bytes 12488 | tf_op jit(solution)/shard_map/ppermute | solution.py:18
  94.2 3.3 %fusion.12 = f32[8,129,256]{2,0,1:T(8,128)} fusion(f32[8,128,256]{2,0,1:T(8,128)S(1)} %fusion.14, f32[8,1,256]{2,0,1:T(8,128)S(1)} %collective-permute-done.8, f32[8,1,256]{2,0,1:T(8,128)S(1)} %collective-permute-done.9, f32[8,130,258]{2,0,1:T(8,128)} %copy-done.5, f32[8,130,258]{2,0,1:T(8,128)S(1)} %fusion), kind=kLoop, calls=%fused_computation.33 | loop fusion | flops 2377728 | bytes 5292032 | tf_op jit(solution)/shard_map/mul | solution.py:34
  99.9 2.8 %fusion.3 = f32[8,128,257]{2,0,1:T(8,128)S(1)} fusion(f32[8,130,1]{2,0,1:T(8,128)} %copy.92, f32[8,1,256]{2,0,1:T(8,128)S(1)} %collective-permute-done.9, f32[8,128,256]{2,0,1:T(8,128)S(1)} %fusion.14, f32[8,1,256]{2,0,1:T(8,128)S(1)} %collective-permute-done.8, f32[8,130,1]{2,0,1:T(8,128)} %copy.90, f32[8,130,258]{2,0,1:T(8,128)} %copy-done.1, ...), kind=kLoop, calls=%fused_computation.9 | loop fusion | flops 3421184 | bytes 5283968 | tf_op jit(solution)/shard_map/mul | solution.py:30
  104.4 15.7 %all_gather.9 = f32[128,1024]{1,0:T(8,128)S(1)} all-gather(f32[128,256]{1,0:T(8,128)S(1)} %add.126), channel_id=1, replica_groups=mesh['gy'=8,'gx'=4] {'gx'}, dimensions={1}, use_global_device_ids=true | all-gather | bytes 655360 | tf_op jit(solution)/shard_map/all_gather | solution.py:97
  120.2 1.9 collective-permute-start.12
  122.1 4.8 %collective-permute-start.13 = (f32[1,1024]{1,0:T(1,128)S(1)}, f32[1,1024]{1,0:T(1,128)S(1)}, u32[]{:S(2)}, u32[]{:S(2)}) collective-permute-start(f32[1,1024]{1,0:T(1,128)S(1)} %get-tuple-element.55), channel_id=1, source_target_pairs={{4,0},{8,4},{12,8},{16,12},{20,16},{24,20},{28,24},{5,1},{9,5},{13... | collective-permute-start | bytes 12296 | tf_op jit(solution)/shard_map/ppermute | solution.py:18
  131.1 2.1 concatenate.73
  135.7 13.0 %all-reduce.2 = (f32[]{:T(128)}, f32[]{:T(128)}) all-reduce(f32[]{:T(128)} %get-tuple-element.15, f32[]{:T(128)} %get-tuple-element.14), channel_id=1, replica_groups=mesh['gy'=8,'gx'=4] {'gy'}, use_global_device_ids=true, to_apply=%region_2.3 | all-reduce | flops 2 | bytes 16 | tf_op jit(solution)/shard_map/psum | solution.py:109
  152.1 4.5 %collective-permute-start.15 = (f32[1,1024]{1,0:T(1,128)S(1)}, f32[1,1024]{1,0:T(1,128)S(1)}, u32[]{:S(2)}, u32[]{:S(2)}) collective-permute-start(f32[1,1024]{1,0:T(1,128)S(1)} %get-tuple-element.53), channel_id=1, source_target_pairs={{4,0},{8,4},{12,8},{16,12},{20,16},{24,20},{28,24},{5,1},{9,5},{13... | collective-permute-start | bytes 12296 | tf_op jit(solution)/shard_map/ppermute | solution.py:18
  159.0 2.1 concatenate.75
  162.3 2.2 %multiply_reduce_fusion.2 = (f32[]{:T(128)}, f32[]{:T(128)}, f32[128,1024]{1,0:T(8,128)}) fusion(f32[128,1024]{1,0:T(8,128)S(1)} %copy-done.7, f32[128,1024]{1,0:T(8,128)S(1)} %all_gather.9, f32[128,1024]{1,0:T(8,128)S(1)} %get-tuple-element.25, f32[]{:T(128)S(6)} %div.31, f32[128,1024]{1,0:T(8,128)S(1)} %copy.96, f32[130,1026]{1,0:T(8,128)S(1)} %mul.198, ...), kind=kLoop, calls=%fused_computation.88 | loop fusion | flops 2359294 | bytes 7340044 | tf_op jit(solution)/shard_map/reduce_sum | solution.py:69
  164.6 15.1 %all-reduce.1 = (f32[]{:T(128)}, f32[]{:T(128)}) all-reduce(f32[]{:T(128)} %get-tuple-element.13, f32[]{:T(128)} %get-tuple-element.12), channel_id=1, replica_groups=mesh['gy'=8,'gx'=4] {'gy'}, use_global_device_ids=true, to_apply=%region_6.7 | all-reduce | flops 2 | bytes 16 | tf_op jit(solution)/shard_map/psum | solution.py:109
  184.1 2.1 add_divide_fusion
  187.0 2.1 collective-permute-start.16
  189.0 4.5 %collective-permute-start.17 = (f32[1,1024]{1,0:T(1,128)S(1)}, f32[1,1024]{1,0:T(1,128)S(1)}, u32[]{:S(2)}, u32[]{:S(2)}) collective-permute-start(f32[1,1024]{1,0:T(1,128)S(1)} %get-tuple-element.51), channel_id=1, source_target_pairs={{4,0},{8,4},{12,8},{16,12},{20,16},{24,20},{28,24},{5,1},{9,5},{13... | collective-permute-start | bytes 12296 | tf_op jit(solution)/shard_map/ppermute | solution.py:18
  193.6 2.5 %copy.99 = f32[8,128,256]{2,1,0:T(8,128)} copy(f32[8,128,256]{2,0,1:T(8,128)} %get-tuple-element.27) | data formatting | bytes 2097152
  197.1 2.2 concatenate.77
  202.0 13.8 %all-reduce = (f32[]{:T(128)}, f32[]{:T(128)}) all-reduce(f32[]{:T(128)} %get-tuple-element.11, f32[]{:T(128)} %get-tuple-element.10), channel_id=1, replica_groups=mesh['gy'=8,'gx'=4] {'gy'}, use_global_device_ids=true, to_apply=%region_10.11 | all-reduce | flops 2 | bytes 16 | tf_op jit(solution)/shard_map/psum | solution.py:109
  (132 shorter events, 48.3 us)
Async XLA Ops:
  0.6 1.3 copy-start.21
  4.4 3.7 %copy-start.2 = (f32[8,128,256]{2,1,0:T(8,128)S(1)}, f32[8,128,256]{2,1,0:T(8,128)}, u32[]{:S(2)}) copy-start(f32[8,128,256]{2,1,0:T(8,128)} %param.7) | copy-start | bytes 3145732
  5.4 6.0 %copy-start.23 = (f32[128,256]{1,0:T(8,128)S(1)}, f32[128,256]{1,0:T(8,128)}, u32[]{:S(2)}) copy-start(f32[128,256]{1,0:T(8,128)} %param.13) | copy-start | bytes 393220
  5.4 30.7 %collective-permute-start = (f32[3,8,1,256]{3,1,2,0:T(8,128)S(1)}, f32[3,8,1,256]{3,1,2,0:T(8,128)S(1)}, u32[]{:S(2)}, u32[]{:S(2)}) collective-permute-start(f32[3,8,1,256]{3,1,2,0:T(8,128)S(1)} %get-tuple-element.32), channel_id=1, source_target_pairs={{0,4},{4,8},{8,12},{12,16},{16,20},{20,24},{24,28},{28,0},{1,5},{5... | collective-permute-start | bytes 73736 | tf_op jit(solution)/shard_map/ppermute | solution.py:17
  5.4 30.7 %collective-permute-start.1 = (f32[3,8,1,256]{3,1,2,0:T(8,128)S(1)}, f32[3,8,1,256]{3,1,2,0:T(8,128)S(1)}, u32[]{:S(2)}, u32[]{:S(2)}) collective-permute-start(f32[3,8,1,256]{3,1,2,0:T(8,128)S(1)} %get-tuple-element.33), channel_id=1, source_target_pairs={{4,0},{8,4},{12,8},{16,12},{20,16},{24,20},{28,24},{0,28},{5,1},{9... | collective-permute-start | bytes 73736 | tf_op jit(solution)/shard_map/ppermute | solution.py:18
  8.7 17.7 %collective-permute-start.4 = (f32[8,1,256]{2,0,1:T(8,128)S(1)}, f32[8,1,256]{2,0,1:T(8,128)S(1)}, u32[]{:S(2)}, u32[]{:S(2)}) collective-permute-start(f32[8,1,256]{2,0,1:T(8,128)S(1)} %get-tuple-element.41), channel_id=1, source_target_pairs={{0,4},{4,8},{8,12},{12,16},{16,20},{20,24},{24,28},{28,0},{1,5},{5... | collective-permute-start | bytes 24584 | tf_op jit(solution)/shard_map/ppermute | solution.py:17
  9.6 18.6 %collective-permute-start.5 = (f32[8,1,256]{2,0,1:T(8,128)S(1)}, f32[8,1,256]{2,0,1:T(8,128)S(1)}, u32[]{:S(2)}, u32[]{:S(2)}) collective-permute-start(f32[8,1,256]{2,0,1:T(8,128)S(1)} %get-tuple-element.40), channel_id=1, source_target_pairs={{4,0},{8,4},{12,8},{16,12},{20,16},{24,20},{28,24},{0,28},{5,1},{9... | collective-permute-start | bytes 24584 | tf_op jit(solution)/shard_map/ppermute | solution.py:18
  31.6 16.9 %collective-permute-start.6 = (f32[8,130,1]{1,0,2:T(8,128)S(1)}, f32[8,130,1]{1,0,2:T(8,128)S(1)}, u32[]{:S(2)}, u32[]{:S(2)}) collective-permute-start(f32[8,130,1]{1,0,2:T(8,128)S(1)} %copy.82), channel_id=1, source_target_pairs={{0,1},{1,2},{2,3},{3,0},{4,5},{5,6},{6,7},{7,4},{8,9},{9,10},{10,1... | collective-permute-start | bytes 12488 | tf_op jit(solution)/shard_map/ppermute | solution.py:17
  34.1 14.9 %collective-permute-start.7 = (f32[8,130,1]{1,0,2:T(8,128)S(1)}, f32[8,130,1]{1,0,2:T(8,128)S(1)}, u32[]{:S(2)}, u32[]{:S(2)}) collective-permute-start(f32[8,130,1]{1,0,2:T(8,128)S(1)} %copy.84), channel_id=1, source_target_pairs={{1,0},{2,1},{3,2},{0,3},{5,4},{6,5},{7,6},{4,7},{9,8},{10,9},{11,1... | collective-permute-start | bytes 12488 | tf_op jit(solution)/shard_map/ppermute | solution.py:18
  42.1 8.0 %collective-permute-start.2 = (f32[3,8,130,1]{2,1,3,0:T(8,128)S(1)}, f32[3,8,130,1]{2,1,3,0:T(8,128)S(1)}, u32[]{:S(2)}, u32[]{:S(2)}) collective-permute-start(f32[3,8,130,1]{2,1,3,0:T(8,128)S(1)} %copy.75), channel_id=1, source_target_pairs={{0,1},{1,2},{2,3},{3,0},{4,5},{5,6},{6,7},{7,4},{8,9},{9,10},{10,1... | collective-permute-start | bytes 37448 | tf_op jit(solution)/shard_map/ppermute | solution.py:17
  44.5 7.7 %collective-permute-start.3 = (f32[3,8,130,1]{2,1,3,0:T(8,128)S(1)}, f32[3,8,130,1]{2,1,3,0:T(8,128)S(1)}, u32[]{:S(2)}, u32[]{:S(2)}) collective-permute-start(f32[3,8,130,1]{2,1,3,0:T(8,128)S(1)} %copy.76), channel_id=1, source_target_pairs={{1,0},{2,1},{3,2},{0,3},{5,4},{6,5},{7,6},{4,7},{9,8},{10,9},{11,1... | collective-permute-start | bytes 37448 | tf_op jit(solution)/shard_map/ppermute | solution.py:18
  60.4 3.6 %copy-start.5 = (f32[8,130,258]{2,0,1:T(8,128)}, f32[8,130,258]{2,0,1:T(8,128)S(1)}, u32[]{:S(2)}) copy-start(f32[8,130,258]{2,0,1:T(8,128)S(1)} %get-tuple-element.29) | copy-start | bytes 3219844
  60.5 2.0 copy-start.11
  60.5 2.5 %copy-start.19 = (f32[8,130,1]{2,0,1:T(8,128)S(1)}, f32[8,130,1]{2,0,1:T(8,128)}, u32[]{:S(2)}) copy-start(f32[8,130,1]{2,0,1:T(8,128)} %copy.85) | copy-start | bytes 12484
  66.3 20.0 %collective-permute-start.8 = (f32[8,1,256]{2,0,1:T(8,128)S(1)}, f32[8,1,256]{2,0,1:T(8,128)S(1)}, u32[]{:S(2)}, u32[]{:S(2)}) collective-permute-start(f32[8,1,256]{2,0,1:T(8,128)S(1)} %get-tuple-element.39), channel_id=1, source_target_pairs={{0,4},{4,8},{8,12},{12,16},{16,20},{20,24},{24,28},{28,0},{1,5},{5... | collective-permute-start | bytes 24584 | tf_op jit(solution)/shard_map/ppermute | solution.py:17
  66.4 19.9 %collective-permute-start.9 = (f32[8,1,256]{2,0,1:T(8,128)S(1)}, f32[8,1,256]{2,0,1:T(8,128)S(1)}, u32[]{:S(2)}, u32[]{:S(2)}) collective-permute-start(f32[8,1,256]{2,0,1:T(8,128)S(1)} %get-tuple-element.38), channel_id=1, source_target_pairs={{4,0},{8,4},{12,8},{16,12},{20,16},{24,20},{28,24},{0,28},{5,1},{9... | collective-permute-start | bytes 24584 | tf_op jit(solution)/shard_map/ppermute | solution.py:18
  88.9 8.6 %collective-permute-start.10 = (f32[8,130,1]{1,0,2:T(8,128)S(1)}, f32[8,130,1]{1,0,2:T(8,128)S(1)}, u32[]{:S(2)}, u32[]{:S(2)}) collective-permute-start(f32[8,130,1]{1,0,2:T(8,128)S(1)} %copy.89), channel_id=1, source_target_pairs={{0,1},{1,2},{2,3},{3,0},{4,5},{5,6},{6,7},{7,4},{8,9},{9,10},{10,1... | collective-permute-start | bytes 12488 | tf_op jit(solution)/shard_map/ppermute | solution.py:17
  90.7 8.0 %collective-permute-start.11 = (f32[8,130,1]{1,0,2:T(8,128)S(1)}, f32[8,130,1]{1,0,2:T(8,128)S(1)}, u32[]{:S(2)}, u32[]{:S(2)}) collective-permute-start(f32[8,130,1]{1,0,2:T(8,128)S(1)} %copy.91), channel_id=1, source_target_pairs={{1,0},{2,1},{3,2},{0,3},{5,4},{6,5},{7,6},{4,7},{9,8},{10,9},{11,1... | collective-permute-start | bytes 12488 | tf_op jit(solution)/shard_map/ppermute | solution.py:18
  99.9 2.8 %copy-start.4 = (f32[8,129,256]{2,0,1:T(8,128)S(1)}, f32[8,129,256]{2,0,1:T(8,128)}, u32[]{:S(2)}) copy-start(f32[8,129,256]{2,0,1:T(8,128)} %fusion.12) | copy-start | bytes 3170308
  99.9 2.8 %copy-start.22 = (s32[128,256]{1,0:T(8,128)S(1)}, s32[128,256]{1,0:T(8,128)}, u32[]{:S(2)}) copy-start(s32[128,256]{1,0:T(8,128)} %param.10) | copy-start | bytes 393220
  99.9 2.8 %copy-start.25 = (f32[8]{0:T(128)S(1)}, f32[8]{0:T(128)}, u32[]{:S(2)}) copy-start(f32[8]{0:T(128)} %param.11) | copy-start | bytes 100
  102.7 1.6 copy-start.24
  104.4 23.5 %copy-start.9 = (f32[4,130,256]{2,1,0:T(8,128)S(1)}, f32[4,130,256]{2,1,0:T(8,128)}, u32[]{:S(2)}) copy-start(f32[4,130,256]{2,1,0:T(8,128)} %copy-done.8) | copy-start | bytes 1597444
  120.2 9.9 %collective-permute-start.12 = (f32[1,1024]{1,0:T(1,128)S(1)}, f32[1,1024]{1,0:T(1,128)S(1)}, u32[]{:S(2)}, u32[]{:S(2)}) collective-permute-start(f32[1,1024]{1,0:T(1,128)S(1)} %get-tuple-element.54), channel_id=1, source_target_pairs={{0,4},{4,8},{8,12},{12,16},{16,20},{20,24},{24,28},{1,5},{5,9},{9,... | collective-permute-start | bytes 12296 | tf_op jit(solution)/shard_map/ppermute | solution.py:17
  122.1 8.0 %collective-permute-start.13 = (f32[1,1024]{1,0:T(1,128)S(1)}, f32[1,1024]{1,0:T(1,128)S(1)}, u32[]{:S(2)}, u32[]{:S(2)}) collective-permute-start(f32[1,1024]{1,0:T(1,128)S(1)} %get-tuple-element.55), channel_id=1, source_target_pairs={{4,0},{8,4},{12,8},{16,12},{20,16},{24,20},{28,24},{5,1},{9,5},{13... | collective-permute-start | bytes 12296 | tf_op jit(solution)/shard_map/ppermute | solution.py:18
  150.2 7.8 %copy-start.6 = (f32[128,1024]{1,0:T(8,128)}, f32[128,1024]{1,0:T(8,128)S(1)}, u32[]{:S(2)}) copy-start(f32[128,1024]{1,0:T(8,128)S(1)} %add_divide_fusion.1) | copy-start | bytes 1572868
  150.2 6.5 %collective-permute-start.14 = (f32[1,1024]{1,0:T(1,128)S(1)}, f32[1,1024]{1,0:T(1,128)S(1)}, u32[]{:S(2)}, u32[]{:S(2)}) collective-permute-start(f32[1,1024]{1,0:T(1,128)S(1)} %get-tuple-element.52), channel_id=1, source_target_pairs={{0,4},{4,8},{8,12},{12,16},{16,20},{20,24},{24,28},{1,5},{5,9},{9,... | collective-permute-start | bytes 12296 | tf_op jit(solution)/shard_map/ppermute | solution.py:17
  152.1 5.9 %collective-permute-start.15 = (f32[1,1024]{1,0:T(1,128)S(1)}, f32[1,1024]{1,0:T(1,128)S(1)}, u32[]{:S(2)}, u32[]{:S(2)}) collective-permute-start(f32[1,1024]{1,0:T(1,128)S(1)} %get-tuple-element.53), channel_id=1, source_target_pairs={{4,0},{8,4},{12,8},{16,12},{20,16},{24,20},{28,24},{5,1},{9,5},{13... | collective-permute-start | bytes 12296 | tf_op jit(solution)/shard_map/ppermute | solution.py:18
  186.9 9.2 %copy-start.18 = (f32[128,1024]{1,0:T(8,128)S(1)}, f32[128,1024]{1,0:T(8,128)}, u32[]{:S(2)}) copy-start(f32[128,1024]{1,0:T(8,128)} %copy-done.17) | copy-start | bytes 1572868
  187.0 9.2 %collective-permute-start.16 = (f32[1,1024]{1,0:T(1,128)S(1)}, f32[1,1024]{1,0:T(1,128)S(1)}, u32[]{:S(2)}, u32[]{:S(2)}) collective-permute-start(f32[1,1024]{1,0:T(1,128)S(1)} %get-tuple-element.50), channel_id=1, source_target_pairs={{0,4},{4,8},{8,12},{12,16},{16,20},{20,24},{24,28},{1,5},{5,9},{9,... | collective-permute-start | bytes 12296 | tf_op jit(solution)/shard_map/ppermute | solution.py:17
  189.0 7.1 %collective-permute-start.17 = (f32[1,1024]{1,0:T(1,128)S(1)}, f32[1,1024]{1,0:T(1,128)S(1)}, u32[]{:S(2)}, u32[]{:S(2)}) collective-permute-start(f32[1,1024]{1,0:T(1,128)S(1)} %get-tuple-element.51), channel_id=1, source_target_pairs={{4,0},{8,4},{12,8},{16,12},{20,16},{24,20},{28,24},{5,1},{9,5},{13... | collective-permute-start | bytes 12296 | tf_op jit(solution)/shard_map/ppermute | solution.py:18
  197.1 3.3 %copy-start.20 = (f32[128,1024]{1,0:T(8,128)S(1)}, f32[128,1024]{1,0:T(8,128)}, u32[]{:S(2)}) copy-start(f32[128,1024]{1,0:T(8,128)} %get-tuple-element.23) | copy-start | bytes 1572868
  (12 other events, 12.4 us)
